TPU v7x, 32 devices: a whole 2x2x4 slice. The times are simulated.
32 devices in a mesh: dp: 4 (over x, core), ep: 8 (over z, y).
Axes of the slice: x: 2, y: 2, z: 4, core: 2. Of those that a mesh axis runs over, the one named last changes fastest.
Arguments:
- tokens: bfloat16 [4096, 2048], P(('dp', 'ep')), parts along dimension 0, may hold values from -6 to 6
- expert_ids: int32 [4096, 8], P(('dp', 'ep')), parts along dimension 0, may hold values from 0 to 15, all different within a row; in each aligned block of 32 rows (0 to 31, 32 to 63, ...) at most 32 rows name the same one
- gate_nums: int32 [4096, 8], P(('dp', 'ep')), parts along dimension 0, may hold values from 64 to 1023
- w_gate: bfloat16 [16, 2048, 768], P('ep'), may hold values from -0.125 to 0.125
- w_up: bfloat16 [16, 2048, 768], P('ep'), may hold values from -0.125 to 0.125
- w_down: bfloat16 [16, 768, 2048], P('ep'), may hold values from -0.21875 to 0.21875
Outputs:
- mixed: bfloat16 [4096, 2048], P(('dp', 'ep')), parts along dimension 0
There are 4 independent parts, one for each index of `dp`. A program takes and returns all parts, laid end to end along the dimension named above; an argument that names none is the same for every part. Nothing has to cross between parts.
Inputs may be any that keep to these rules, and one draw needn't show every extreme that they name: `expert_ids`: each row names 8 different experts. In every aligned block of 32 rows no expert is named by more than 32 rows, a bound that some block reaches.
All inputs are finite; a program needn't handle non-finite values.
Results may differ from a plain program's by a relative error of at most 0.008.
Values may be sent and summed in bfloat16 or wider, within the bound.
A program may use at most 128 MiB of HBM per device.

v0:
```python
import functools

import jax
import jax.numpy as jnp
from jax import lax
from jax.experimental import pallas as pl
from jax.experimental.pallas import tpu as pltpu
from jax.sharding import PartitionSpec as P

denominator = 1024.0
SIDE = 2
LANES = 256
VMEM = 60 * 2**20


def expert_weights(expert_ids, gate_nums, experts):
    gates = gate_nums.astype(jnp.float32) / denominator
    labels = jnp.arange(experts, dtype=jnp.int32)
    onehot = expert_ids[:, :, None] == labels[None, None, :]
    return jnp.sum(jnp.where(onehot, gates[:, :, None], 0.0), axis=1)


def kernel(
    n, local, messages,
    tokens, weights, w_gate, w_up, w_down, out,
    rows, factors, gate, up, down, hidden, part, from_side, from_line,
    load_sem, weight_send, weight_recv, line_send, line_recv, side_send, side_recv,
    back_side_send, back_side_recv, back_line_send, back_line_recv,
):
    depth = n // SIDE
    me = lax.axis_index("ep")
    z, y = me // SIDE, me % SIDE
    other = SIDE - 1 - y
    partner = z * SIDE + other
    ff = w_gate.shape[2]
    count = tokens.shape[0]
    width = tokens.shape[1]
    last = depth - 1
    late = [m for m, (_, _, side, _) in enumerate(messages) if not side]
    early = [m for m, (_, _, side, _) in enumerate(messages) if side]
    late_back = [m for m, (_, _, _, side) in enumerate(messages) if not side]
    early_back = [m for m, (_, _, _, side) in enumerate(messages) if side]
    cuts = [pl.ds(start, size) for start, size, _, _ in messages]

    def remote(source, target, send, recv, device):
        return pltpu.make_async_remote_copy(
            src_ref=source, dst_ref=target, send_sem=send, recv_sem=recv,
            device_id={"ep": device}, device_id_type=pl.DeviceIdType.MESH,
        )

    own = pltpu.make_async_copy(tokens, rows.at[z, y], load_sem.at[0])
    own.start()
    loads = []
    for e in range(local):
        cut = pl.ds(e * ff, ff)
        loads.append(pltpu.make_async_copy(w_gate.at[e], gate.at[e], load_sem.at[1 + 3 * e]))
        loads.append(pltpu.make_async_copy(w_up.at[e], up.at[e], load_sem.at[2 + 3 * e]))
        loads.append(pltpu.make_async_copy(w_down.at[e], down.at[cut], load_sem.at[3 + 3 * e]))
    for load in loads:
        load.start()

    barrier = pltpu.get_barrier_semaphore()
    for k in range(1, n):
        pl.semaphore_signal(
            barrier, inc=1, device_id={"ep": (me + k) % n}, device_id_type=pl.DeviceIdType.MESH
        )
    pl.semaphore_wait(barrier, n - 1)
    own.wait()

    def side_copy(o, row, m):
        ref = rows.at[o, row, cuts[m]]
        return remote(ref, ref, side_send.at[o, m], side_recv.at[o, m], partner)

    def line_copy(o, row, m, way):
        ref = rows.at[o, row, cuts[m]]
        there = me + SIDE * (1 - 2 * way)
        return remote(
            ref, ref, line_send.at[way, o, row, m], line_recv.at[o, row, m], there
        )

    def onward(o, row, m, act):
        @pl.when((o <= z) & (z < last))
        def _():
            act(line_copy(o, row, m, 0))

        @pl.when((o >= z) & (z > 0))
        def _():
            act(line_copy(o, row, m, 1))

    def start(copy):
        copy.start()

    def wait_send(copy):
        copy.wait_send()

    def weight_copy(k):
        there = (me + k) % n
        return remote(weights.at[there], factors.at[me], weight_send.at[k], weight_recv.at[me], there)

    def back_side(o, m):
        return remote(
            part.at[o, other, cuts[m]], from_side.at[o, cuts[m]],
            back_side_send.at[o, m], back_side_recv.at[o, m], partner,
        )

    def back_line(o, row, m, way):
        there = me + SIDE * (1 - 2 * way)
        return remote(
            part.at[o, row, cuts[m]], from_line.at[way, o, row, cuts[m]],
            back_line_send.at[o, row, m], back_line_recv.at[way, o, row, m], there,
        )

    def each_back(o, row, m, act):
        @pl.when(o > z)
        def _():
            act(back_line(o, row, m, 0))

        @pl.when(o < z)
        def _():
            act(back_line(o, row, m, 1))

    for m in early:
        side_copy(z, y, m).start()
    for k in range(1, n):
        weight_copy(k).start()
    for m in late:
        onward(z, y, m, start)
        side_copy(z, y, m).start()
    for m in early:
        onward(z, y, m, start)
    factors[me] = weights[me]

    @pl.when(z == 0)
    def _():
        from_line[0] = jnp.zeros_like(from_line[0])

    @pl.when(z == last)
    def _():
        from_line[1] = jnp.zeros_like(from_line[1])

    for m in early:
        side_copy(z, other, m).wait_recv()
        onward(z, other, m, start)

    turn = 1 - 2 * (z // (depth // 2))
    pairs = jnp.minimum(z, last - z)
    middle = jnp.minimum(pairs, 1)

    def nearest(s):
        both = z + turn * ((s + 1) // 2) * (2 * (s % 2) - 1)
        single = z + turn * (s - pairs)
        return jnp.where(s <= 2 * pairs, both, single)

    def rotation(s):
        return (z + turn * s + depth) % depth

    def gather(o):
        for m in late:
            line_copy(o, y, m, 0).wait_recv()
            onward(o, y, m, start)
            side_copy(o, y, m).start()
        for m in early:
            for row in range(SIDE):
                line_copy(o, row, m, 0).wait_recv()
                onward(o, row, m, start)

    gather(nearest(1))

    @pl.when(middle == 1)
    def _():
        gather(nearest(2))

    for load in loads:
        load.wait()
    for k in range(1, n):
        source = (me + k) % n
        remote(
            factors.at[source], factors.at[source], weight_send.at[k], weight_recv.at[source], partner
        ).wait_recv()

    def arrive(o, row, m):
        @pl.when((o >= z) & (z > 0))
        def _():
            back_line(o, row, m, 0).wait_recv()

        @pl.when((o <= z) & (z < last))
        def _():
            back_line(o, row, m, 1).wait_recv()

    def wide(ref):
        return ref[...].astype(jnp.float32)

    def pass_back(o):
        way = (last + z - o) // depth
        for m in early_back:
            for row in range(SIDE):
                arrive(o, row, m)
                total = wide(part.at[o, row, cuts[m]]) + wide(from_line.at[way, o, row, cuts[m]])
                part[o, row, cuts[m]] = total.astype(part.dtype)
                each_back(o, row, m, start)
        for m in late_back:
            back_side(o, m).wait_recv()
            arrive(o, y, m)
            total = wide(part.at[o, y, cuts[m]]) + wide(from_line.at[way, o, y, cuts[m]])
            total = total + wide(from_side.at[o, cuts[m]])
            part[o, y, cuts[m]] = total.astype(part.dtype)
            each_back(o, y, m, start)

    def step(s, carry):
        o = nearest(s)
        for m in late:
            side_copy(o, other, m).wait_recv()
        scale = jnp.concatenate([factors[o * SIDE + i].T for i in range(SIDE)], axis=0)
        for e in range(local):
            column = scale[:, e : e + 1]

            def tile(t, carry):
                cut = pl.ds(pl.multiple_of(t * LANES, LANES), LANES)
                block = rows[o].reshape(SIDE * count, width)
                g = jnp.dot(block, gate[e, :, cut], preferred_element_type=jnp.float32)
                u = jnp.dot(block, up[e, :, cut], preferred_element_type=jnp.float32)
                h = g / (1.0 + jnp.exp(-g)) * u * column
                place = pl.ds(pl.multiple_of(e * ff + t * LANES, LANES), LANES)
                hidden[:, place] = h.astype(jnp.bfloat16)
                return carry

            lax.fori_loop(0, ff // LANES, tile, 0, unroll=True)

        def spread(t, carry):
            cut = pl.ds(pl.multiple_of(t * LANES, LANES), LANES)
            result = jnp.dot(hidden[...], down[:, cut], preferred_element_type=jnp.float32)
            part[o, :, :, cut] = result.astype(jnp.bfloat16).reshape(SIDE, count, LANES)
            return carry

        lax.fori_loop(0, width // LANES, spread, 0, unroll=True)

        @pl.when(s > 0)
        def _():
            for m in late_back:
                back_side(o, m).start()

        @pl.when(s + 2 + middle < depth)
        def _():
            gather(nearest(s + 2 + middle))

        @pl.when((s >= 2) & (middle == 0))
        def _():
            pass_back(rotation(s - 1))

        return carry

    lax.fori_loop(0, depth, step, 0)
    for m in late_back:
        back_side(z, m).start()

    def rest(s, carry):
        pass_back(rotation(s))
        return carry

    lax.fori_loop(1 + (1 - middle) * (depth - 2), depth, rest, 0)

    def collected(row, m):
        arrive(z, row, m)
        total = wide(part.at[z, row, cuts[m]])
        return total + wide(from_line.at[0, z, row, cuts[m]]) + wide(from_line.at[1, z, row, cuts[m]])

    for m in early_back:
        part[z, other, cuts[m]] = collected(other, m).astype(part.dtype)
        back_side(z, m).start()
    for m in late_back + early_back:
        total = collected(y, m)
        back_side(z, m).wait_recv()
        out[cuts[m]] = (total + wide(from_side.at[z, cuts[m]])).astype(out.dtype)

    for k in range(1, n):
        weight_copy(k).wait_send()
    for m in early:
        side_copy(z, y, m).wait_send()
    for m in early_back:
        back_side(z, m).wait_send()

    def settle(o, carry):
        for m in late:
            side_copy(o, y, m).wait_send()
            onward(o, y, m, wait_send)
        for m in late_back:
            back_side(o, m).wait_send()
            each_back(o, y, m, wait_send)
        for row in range(SIDE):
            for m in early:
                onward(o, row, m, wait_send)
            for m in early_back:
                each_back(o, row, m, wait_send)
        return carry

    lax.fori_loop(0, depth, settle, 0)


def fused(tokens, expert_ids, gate_nums, w_gate, w_up, w_down, n):
    count, width = tokens.shape
    local, _, ff = w_gate.shape
    depth = n // SIDE
    weight = expert_weights(expert_ids, gate_nums, local * n)
    pad = -local % 8
    weights = jnp.pad(weight.T.reshape(n, local, count), ((0, 0), (0, pad), (0, 0)))
    unit = count // 8
    messages = [(0 * unit, 2 * unit, False, False), (2 * unit, 2 * unit, False, False), (4 * unit, 2 * unit, False, False), (6 * unit, 1 * unit, False, False), (7 * unit, 1 * unit, True, False)]
    size = len(messages)
    kind = tokens.dtype
    dma = pltpu.SemaphoreType.DMA
    vmem = pl.BlockSpec(memory_space=pltpu.VMEM)
    hbm = pl.BlockSpec(memory_space=pl.ANY)
    return pl.pallas_call(
        functools.partial(kernel, n, local, messages),
        out_shape=jax.ShapeDtypeStruct((count, width), kind),
        in_specs=[hbm, vmem, hbm, hbm, hbm],
        out_specs=vmem,
        scratch_shapes=[
            pltpu.VMEM((depth, SIDE, count, width), kind),
            pltpu.VMEM((n, local + pad, count), jnp.float32),
            pltpu.VMEM((local, width, ff), kind),
            pltpu.VMEM((local, width, ff), kind),
            pltpu.VMEM((local * ff, width), kind),
            pltpu.VMEM((SIDE * count, local * ff), kind),
            pltpu.VMEM((depth, SIDE, count, width), kind),
            pltpu.VMEM((depth, count, width), kind),
            pltpu.VMEM((2, depth, SIDE, count, width), kind),
            dma((1 + 3 * local,)),
            dma((n,)), dma((n,)),
            dma((2, depth, SIDE, size)), dma((depth, SIDE, size)),
            dma((depth, size)), dma((depth, size)),
            dma((depth, size)), dma((depth, size)),
            dma((depth, SIDE, size)), dma((2, depth, SIDE, size)),
        ],
        compiler_params=pltpu.CompilerParams(
            collective_id=0, has_side_effects=True, vmem_limit_bytes=VMEM
        ),
    )(tokens, weights, w_gate, w_up, w_down)


def plain(tokens, expert_ids, gate_nums, w_gate, w_up, w_down, n):
    weight = expert_weights(expert_ids, gate_nums, w_gate.shape[0] * n)
    weights = lax.all_to_all(weight, "ep", split_axis=1, concat_axis=0, tiled=True)
    rows = lax.all_gather(tokens, "ep", axis=0, tiled=True)
    gate = jnp.einsum("td,xdf->xtf", rows, w_gate, preferred_element_type=jnp.float32)
    up = jnp.einsum("td,xdf->xtf", rows, w_up, preferred_element_type=jnp.float32)
    hidden = (jax.nn.silu(gate) * up * weights.T[:, :, None]).astype(jnp.bfloat16)
    result = jnp.einsum("xtf,xfd->td", hidden, w_down, preferred_element_type=jnp.float32)
    return lax.psum_scatter(
        result.astype(jnp.bfloat16), "ep", scatter_dimension=0, tiled=True
    )


def shards(n, tokens, expert_ids, gate_nums, w_gate, w_up, w_down):
    count, width = tokens.shape
    local, _, ff = w_gate.shape
    held = 5 * n * count * width + 3 * local * width * ff + 2 * count * local * ff
    fits = 2 * held < VMEM - 4 * 2**20
    shaped = n % (2 * SIDE) == 0 and count % 128 == 0 and ff % LANES == 0 and width % LANES == 0
    plan = fused if fits and shaped else plain
    return plan(tokens, expert_ids, gate_nums, w_gate, w_up, w_down, n)


def solution(mesh):
    placed = (
        P(("dp", "ep"), None),
        P(("dp", "ep"), None),
        P(("dp", "ep"), None),
        P("ep", None, None),
        P("ep", None, None),
        P("ep", None, None),
    )
    return jax.shard_map(
        functools.partial(shards, mesh.shape["ep"]),
        mesh=mesh, in_specs=placed, out_specs=P(("dp", "ep"), None), check_vma=False,
    )
```

profile of v0, /device:TPU:0, one launch (start us, length us, event | category | flops | bytes accessed | tf_op | source)
XLA Modules:
  0.0 106.4 jit_solution(2916803801547462965)
XLA Ops:
  0.0 0.7 convert_multiply_fusion
  0.7 0.7 select_reduce_fusion
  1.4 0.6 pad.4.weights
  2.0 102.5 %shard_map.64 = bf16[128,2048]{1,0:T(8,128)(2,1)} custom-call(bf16[128,2048]{1,0:T(8,128)(2,1)} %tokens.1, f32[8,8,128]{2,1,0:T(8,128)} %pad.4.weights, bf16[2,2048,768]{2,1,0:T(8,128)(2,1)} %w_gate.1, bf16[2,2048,768]{2,1,0:T(8,128)(2,1)} %w_up.1, bf16[2,768,2048]{2,1,0:T(8,128)(2,1)} %w_down.1), custom_call_target="tpu_custom_call" | custom-call | tf_op jit(solution)/shard_map/pallas_call | solution.py:313
  104.5 1.9 %copy.10 = bf16[128,2048]{1,0:T(8,128)(2,1)} copy(bf16[128,2048]{1,0:T(8,128)(2,1)} %shard_map.64) | data formatting | bytes 1048576
where the time goes:
time: 107 us; the launch traced here: 106 us
  Pallas kernels  102 us (95%)
  local copies, waits for them, and re-layouts  2.5 us (2%)
  other arithmetic  1.39 us (1%)
    pallas_call x1, Pallas kernels, fused(): pl.pallas_call(functools.partial(kernel, n, local, messages), out_shape=j...  102 us

commit v1 on v0

v1 whole, which is shorter than its diff:
```python
import functools

import jax
import jax.numpy as jnp
from jax import lax
from jax.experimental import pallas as pl
from jax.experimental.pallas import tpu as pltpu
from jax.sharding import PartitionSpec as P

denominator = 1024.0
SIDE = 2
LANES = 256
VMEM = 60 * 2**20

AWAY, HOME, ACROSS = 0, 1, 2
UNITS = 8
PIECES = 4
ROUNDS = (
    ((0, 0), (1, 0), (2, 0), (2, 1), (0, 1), (3, 0), (3, 1), (1, 1)),
    ((1, 0), (2, 1), (0, 1), (0, 0), (2, 0), (1, 1), (3, 0), (3, 1)),
)
SENDS = (
    (
        (10000, 10002, 10010, 10022, 10020, 10032, 10030, 11002, 10040, 11012, 10050, 11022, 10060, 10042,
         10070, 10052, 11100, 12002, 10130, 12012, 12022, 10150),
        (),
        (12100, 11032),
        (),
        (11042, 20100, 20110, 12032, 20120, 12042),
        (12052,),
        (),
        (),
        (21100, 21132, 21110),
        (),
        (21120, 12062),
        (),
        (22112, 22000, 22122, 21000, 22132, 12072, 22010, 13002, 22020, 13012, 21010, 22030, 13022, 21020),
        (),
        (13042,),
        (),
        (21030, 22040, 22152),
        (22172,),
        (22100,),
        (),
        (20142,),
        (20152,),
        (22050, 20162),
        (),
        (22070, 23130, 23102),
        (23030,),
        (23122,),
        (),
        (23160, 23170, 11062, 11072, 23000, 23142, 23020, 23060, 23112, 23152),
        (),
        (23040, 20132),
        (),
        (23010, 20172, 23070, 23050, 22162, 21142, 22140, 21152, 30000, 21162, 30020, 22060, 21172, 30030,
         21040, 30040, 21050, 30010, 21060, 30050, 21070, 30060, 30070),
    ),
    (
        (11000, 11001, 11012, 11010, 11011, 11022, 11020, 11021, 11032, 11030, 12001, 10002, 11120, 12011,
         10012, 11130, 12021, 10022, 12012, 10100, 12031, 11040, 10111, 10042, 11050, 11031, 11042, 11060,
         11041, 10062, 11070, 12041, 10072, 10000, 12042, 12051),
        (10010, 12052),
        (10161,),
        (11062,),
        (10150, 10171, 10020, 12061, 11072, 10030, 12071, 13012, 11160, 13151, 13001, 13022, 11170, 10040,
         13011, 13032, 13021, 21102, 10050, 21110),
        (13131, 10060, 13031, 21122),
        (13042,),
        (10070, 13041),
        (22152, 22172),
        (12150,),
        (13051,),
        (),
        (13062, 13061),
        (),
        (13072, 13071),
        (),
        (20110, 20102, 20122),
        (13161,),
        (20142, 11151),
        (13171, 20152),
        (11051, 22130, 22030),
        (),
        (11061,),
        (22112,),
        (11071, 22102),
        (22122,),
        (21141, 22050),
        (),
        (22070, 22000, 23102, 23111),
        (23122, 21161),
        (22010,),
        (23132, 20131),
        (22020, 23142, 20171, 23160, 31000, 23152, 22161, 31010, 23172, 23000, 31020, 23030, 23020, 20162,
         21132, 20001, 21152, 23040, 20021, 21172, 23010, 20031, 23060, 23050, 20041, 31030, 23070, 20011,
         22142, 20051, 22060, 20061, 22040, 20071, 31050, 31060, 31040, 31070),
    ),
)


def expert_weights(expert_ids, gate_nums, experts):
    gates = gate_nums.astype(jnp.float32) / denominator
    labels = jnp.arange(experts, dtype=jnp.int32)
    onehot = expert_ids[:, :, None] == labels[None, None, :]
    return jnp.sum(jnp.where(onehot, gates[:, :, None], 0.0), axis=1)


def digits(code):
    return code // 10000, code // 1000 % 10, code // 100 % 10, code // 10 % 10, code % 10


def script(depth):
    acts, came = [], [{} for _ in SENDS]
    for role, pieces in enumerate(SENDS):
        seen, mine = set(), []
        for index, piece in enumerate(pieces):
            found = []

            def need(o, r, u):
                if (o, r) != (role, 0) and (o, r, u) not in seen:
                    seen.add((o, r, u))
                    found.append((0, o, r, u, ACROSS))

            for code in piece:
                kind, o, r, u, way = digits(code)
                if kind == 1:
                    need(o, r, u)
                found.append((kind, o, r, u, way))
                if kind != 2:
                    continue
                there, key = role + (way == AWAY) - (way == HOME), (o, r, u)
                if way == ACROSS:
                    key = (o, 1 - r, u)
                if there == depth // 2:
                    there, key, way = role, (depth - 1 - o, r, u), HOME
                came[there].setdefault(key, []).append(way)
            if index % PIECES == 0 and index < len(ROUNDS[role]) * PIECES:
                o, h = ROUNDS[role][index // PIECES]
                for r in range(SIDE):
                    for u in range(h * UNITS // 2, (h + 1) * UNITS // 2):
                        need(o, r, u)
            mine.append(found)
        acts.append(mine)
    return acts, came


def kernel(
    n, local,
    ids, nums, tokens, w_gate, w_up, w_down, out,
    rows, weights, factors, columns, gate, up, down, hidden, part, line, side,
    load_sem, weight_send, weight_recv, token_send, token_recv, result_send, line_recv, side_recv,
):
    depth = n // SIDE
    me = lax.axis_index("ep")
    z, y = me // SIDE, me % SIDE
    flip = z // (depth // 2)
    place = z + flip * (depth - 1 - 2 * z)
    count, width = tokens.shape
    ff = w_gate.shape[2]
    size = count // UNITS
    half = count // 2
    spots = depth * SIDE * UNITS
    acts, came = script(depth)
    steps = len(ROUNDS[0])

    def owner_of(o):
        return o + flip * (depth - 1 - 2 * o)

    def row_of(r):
        return y if r == 0 else 1 - y

    def offset(o, r, u):
        return owner_of(o) * SIDE * count + u * size // half * count + row_of(r) * half + u * size % half

    def spot(o, r, u):
        return (owner_of(o) * SIDE + row_of(r)) * UNITS + u

    def cut(start, extent=size):
        return pl.ds(pl.multiple_of(start, size), extent)

    def heading(way):
        return flip if way == AWAY else 1 - flip

    def device(way):
        return z * SIDE + 1 - y if way == ACROSS else me + SIDE * (1 - 2 * heading(way))

    def remote(source, target, send, recv, there):
        return pltpu.make_async_remote_copy(
            src_ref=source, dst_ref=target, send_sem=send, recv_sem=recv,
            device_id={"ep": there}, device_id_type=pl.DeviceIdType.MESH,
        )

    def token_copy(o, r, u, way):
        ref = rows.at[cut(offset(o, r, u))]
        return remote(ref, ref, token_send.at[way], token_recv.at[spot(o, r, u)], device(way))

    def landing(o, r, u, way):
        if way == ACROSS:
            return side.at[cut(owner_of(o) * count + u * size)], side_recv.at[owner_of(o) * UNITS + u]
        start = heading(way) * (depth * SIDE * count) + offset(o, r, u)
        return line.at[cut(start)], line_recv.at[heading(way) * spots + spot(o, r, u)]

    def result_copy(o, r, u, way):
        target, recv = landing(o, r, u, way)
        return remote(part.at[cut(offset(o, r, u))], target, result_send.at[way], recv, device(way))

    own = []
    for h in range(2):
        start = z * SIDE * count + h * count + y * half
        own.append(
            pltpu.make_async_copy(tokens.at[pl.ds(h * half, half)], rows.at[cut(start, half)], load_sem.at[h])
        )
    loads = []
    for e in range(local):
        loads.append(pltpu.make_async_copy(w_gate.at[e], gate.at[e], load_sem.at[2 + 3 * e]))
        loads.append(pltpu.make_async_copy(w_up.at[e], up.at[e], load_sem.at[3 + 3 * e]))
    for e in range(local):
        loads.append(pltpu.make_async_copy(w_down.at[e], down.at[pl.ds(e * ff, ff)], load_sem.at[4 + 3 * e]))
    for load in own + loads:
        load.start()

    barrier = pltpu.get_barrier_semaphore()
    for k in range(1, n):
        pl.semaphore_signal(
            barrier, inc=1, device_id={"ep": (me + k) % n}, device_id_type=pl.DeviceIdType.MESH
        )

    gates = nums[...].astype(jnp.float32) / denominator
    lanes = lax.broadcasted_iota(jnp.int32, weights.shape[1:], 0)
    for d in range(n):
        block = jnp.zeros(weights.shape[1:], jnp.float32)
        for e in range(local):
            chosen = jnp.sum(jnp.where(ids[...] == d * local + e, gates, 0.0), axis=0, keepdims=True)
            block = jnp.where(lanes == e, chosen, block)
        weights[d] = block
    factors[me] = weights[me]

    pl.semaphore_wait(barrier, n - 1)
    for load in own:
        load.wait()

    def act(role, kind, o, r, u, way):
        if kind == 0:
            token_copy(o, r, u, way).wait_recv()
            return
        if kind == 1:
            token_copy(o, r, u, way).start()
            return
        if kind == 3:
            o, r = role, 0
        mine = part.at[cut(offset(o, r, u))]
        ways = came[role].get((o, r, u), [])
        if ways:
            total = mine[...].astype(jnp.float32)
            for source in ways:
                target, recv = landing(o, r, u, source)
                remote(target, target, result_send.at[source], recv, device(source)).wait_recv()
                total = total + target[...].astype(jnp.float32)
            if kind == 2:
                mine[...] = total.astype(part.dtype)
        if kind == 2:
            result_copy(o, r, u, way).start()
        else:
            out[pl.ds(u * size, size)] = total.astype(out.dtype)

    def talk(p, i):
        for role, pieces in enumerate(acts):
            for step in range(steps):
                piece = pieces[step * PIECES + p]

                def body(role=role, piece=piece):
                    for action in piece:
                        act(role, *action)

                if piece:
                    pl.when((place == role) & (i == step))(body)

    def pick(i, which):
        found = jnp.int32(0)
        for role, rounds in enumerate(ROUNDS):
            for step, entry in enumerate(rounds):
                if entry[which]:
                    found = found + jnp.where((place == role) & (i == step), entry[which], 0)
        return found

    def weight_copy(k):
        there = (me + k) % n
        return remote(weights.at[there], factors.at[me], weight_send.at[0], weight_recv.at[me], there)

    for k in range(1, n):
        weight_copy(k).start()

    def ready():
        for k in range(1, n):
            source = (me + k) % n
            there = factors.at[source]
            remote(there, there, weight_send.at[0], weight_recv.at[source], source).wait_recv()
        for d in range(n):
            turned = factors[d].T
            for h in range(2):
                start = d // SIDE * SIDE * count + h * count + d % SIDE * half
                columns[pl.ds(start, half)] = turned[h * half : (h + 1) * half]

    def project(e, base):
        column = columns[cut(base, count), e : e + 1]

        def tile(t, carry):
            at = pl.ds(pl.multiple_of(t * LANES, LANES), LANES)
            block = rows[cut(base, count)]
            g = jnp.dot(block, gate[e, :, at], preferred_element_type=jnp.float32)
            v = jnp.dot(block, up[e, :, at], preferred_element_type=jnp.float32)
            h = g / (1.0 + jnp.exp(-g)) * v * column
            hidden[:, pl.ds(pl.multiple_of(e * ff + t * LANES, LANES), LANES)] = h.astype(jnp.bfloat16)
            return carry

        lax.fori_loop(0, ff // LANES, tile, 0, unroll=True)

    def spread(low, high, base):
        def tile(t, carry):
            at = pl.ds(pl.multiple_of(t * LANES, LANES), LANES)
            result = jnp.dot(hidden[...], down[:, at], preferred_element_type=jnp.float32)
            part[cut(base, count), at] = result.astype(jnp.bfloat16)
            return carry

        lax.fori_loop(low, high, tile, 0, unroll=True)

    def step(i, carry):
        o, h = pick(i, 0), pick(i, 1)
        base = owner_of(o) * SIDE * count + h * count
        tiles = width // LANES
        for p in range(PIECES):
            talk(p, i)

            @pl.when(i == 0)
            def _():
                if p == 0:
                    ready()
                for load in loads[2 * p : 2 * p + 2] if p < local else loads[2 * local :] if p == local else []:
                    load.wait()

            if p < local:
                project(p, base)
            else:
                share = tiles // (PIECES - local)
                spread((p - local) * share, (p - local + 1) * share, base)
        return carry

    lax.fori_loop(0, steps, step, 0)

    def ending(role):
        for piece in acts[role][steps * PIECES :]:
            for action in piece:
                act(role, *action)
        for way in (AWAY, HOME, ACROSS):
            for kind, sems in ((1, token_send), (2, result_send)):
                sent = sum(a[0] == kind and a[4] == way for piece in acts[role] for a in piece)
                if sent:
                    all_of = rows.at[pl.ds(0, sent * size)]
                    remote(all_of, all_of, sems.at[way], token_recv.at[0], device(way)).wait_send()

    for role in range(len(acts)):
        pl.when(place == role)(functools.partial(ending, role))
    given = weights.at[pl.ds(0, n - 1)]
    remote(given, given, weight_send.at[0], weight_recv.at[0], device(ACROSS)).wait_send()


def fused(tokens, expert_ids, gate_nums, w_gate, w_up, w_down, n):
    count, width = tokens.shape
    local, _, ff = w_gate.shape
    depth = n // SIDE
    everyone = n * count
    kind = tokens.dtype
    dma = pltpu.SemaphoreType.DMA
    vmem = pl.BlockSpec(memory_space=pltpu.VMEM)
    hbm = pl.BlockSpec(memory_space=pl.ANY)
    return pl.pallas_call(
        functools.partial(kernel, n, local),
        out_shape=jax.ShapeDtypeStruct((count, width), kind),
        in_specs=[vmem, vmem, hbm, hbm, hbm, hbm],
        out_specs=vmem,
        scratch_shapes=[
            pltpu.VMEM((everyone, width), kind),
            pltpu.VMEM((n, 8, count), jnp.float32),
            pltpu.VMEM((n, 8, count), jnp.float32),
            pltpu.VMEM((everyone, 8), jnp.float32),
            pltpu.VMEM((local, width, ff), kind),
            pltpu.VMEM((local, width, ff), kind),
            pltpu.VMEM((local * ff, width), kind),
            pltpu.VMEM((count, local * ff), kind),
            pltpu.VMEM((everyone, width), kind),
            pltpu.VMEM((2 * everyone, width), kind),
            pltpu.VMEM((depth * count, width), kind),
            dma((2 + 3 * local,)),
            dma((1,)), dma((n,)),
            dma((3,)), dma((n * UNITS,)),
            dma((3,)), dma((2 * n * UNITS,)), dma((depth * UNITS,)),
        ],
        compiler_params=pltpu.CompilerParams(
            collective_id=0, has_side_effects=True, vmem_limit_bytes=VMEM
        ),
    )(expert_ids.T, gate_nums.T, tokens, w_gate, w_up, w_down)


def plain(tokens, expert_ids, gate_nums, w_gate, w_up, w_down, n):
    weight = expert_weights(expert_ids, gate_nums, w_gate.shape[0] * n)
    weights = lax.all_to_all(weight, "ep", split_axis=1, concat_axis=0, tiled=True)
    rows = lax.all_gather(tokens, "ep", axis=0, tiled=True)
    gate = jnp.einsum("td,xdf->xtf", rows, w_gate, preferred_element_type=jnp.float32)
    up = jnp.einsum("td,xdf->xtf", rows, w_up, preferred_element_type=jnp.float32)
    hidden = (jax.nn.silu(gate) * up * weights.T[:, :, None]).astype(jnp.bfloat16)
    result = jnp.einsum("xtf,xfd->td", hidden, w_down, preferred_element_type=jnp.float32)
    return lax.psum_scatter(
        result.astype(jnp.bfloat16), "ep", scatter_dimension=0, tiled=True
    )


def shards(n, tokens, expert_ids, gate_nums, w_gate, w_up, w_down):
    count, width = tokens.shape
    local, _, ff = w_gate.shape
    held = 5 * n * count * width + 3 * local * width * ff + 2 * count * local * ff
    fits = 2 * held < VMEM - 4 * 2**20
    planned = n == 2 * SIDE * len(SENDS) and PIECES == local + 2
    shaped = count % (16 * UNITS) == 0 and count % 128 == 0 and ff % LANES == 0 and width % (2 * LANES) == 0
    plan = fused if fits and planned and shaped else plain
    return plan(tokens, expert_ids, gate_nums, w_gate, w_up, w_down, n)


def solution(mesh):
    placed = (
        P(("dp", "ep"), None),
        P(("dp", "ep"), None),
        P(("dp", "ep"), None),
        P("ep", None, None),
        P("ep", None, None),
        P("ep", None, None),
    )
    return jax.shard_map(
        functools.partial(shards, mesh.shape["ep"]),
        mesh=mesh, in_specs=placed, out_specs=P(("dp", "ep"), None), check_vma=False,
    )
```

time: 107 us -> 88.5 us (0.83)
  Pallas kernels: 102 us -> 86.4 us
  other arithmetic: 1.39 us -> 0 us
    pallas_call x1, Pallas kernels: 102 us -> 86.4 us  [fused(): pl.pallas_call(functools.partial(kernel, n, local), out_shape=jax.ShapeDt...]
where the time goes in v1:
time: 88.5 us; the launch traced here: 88.3 us
  Pallas kernels  86.4 us (98%)
  local copies, waits for them, and re-layouts  1.88 us (2%)
    pallas_call x1, Pallas kernels, fused(): pl.pallas_call(functools.partial(kernel, n, local), out_shape=jax.ShapeDt...  86.4 us
    unnamed x1, local copies, waits for them, and re-layouts  1.88 us

profile of v1, /device:TPU:0, one launch (start us, length us, event | category | flops | bytes accessed | tf_op | source)
XLA Modules:
  0.0 88.3 jit_solution(16400337943236781974)
XLA Ops:
  0.0 86.4 %shard_map.64 = bf16[128,2048]{1,0:T(8,128)(2,1)} custom-call(s32[8,128]{1,0:T(8,128)} %bitcast.2, s32[8,128]{1,0:T(8,128)} %bitcast.3, bf16[128,2048]{1,0:T(8,128)(2,1)} %tokens.1, bf16[2,2048,768]{2,1,0:T(8,128)(2,1)} %w_gate.1, bf16[2,2048,768]{2,1,0:T(8,128)(2,1)} %w_up.1, bf16[2,768,2048]{2,1,0:T(8,128)(2,1)} %w_down.1), custom_call_target="tpu_custom_call" | custom-call | tf_op jit(solution)/shard_map/pallas_call | solution.py:378
  86.4 1.9 %copy.8 = bf16[128,2048]{1,0:T(8,128)(2,1)} copy(bf16[128,2048]{1,0:T(8,128)(2,1)} %shard_map.64) | data formatting | bytes 1048576

commit v2 on v1

--- a/solution.py
+++ b/solution.py
@@ -16,86 +16,82 @@
 UNITS = 8
 PIECES = 4
 ROUNDS = (
-    ((0, 0), (1, 0), (2, 0), (2, 1), (0, 1), (3, 0), (3, 1), (1, 1)),
-    ((1, 0), (2, 1), (0, 1), (0, 0), (2, 0), (1, 1), (3, 0), (3, 1)),
+    ((1, 0), (2, 0), (0, 0), (0, 1), (3, 0), (3, 1), (2, 1), (1, 1)),
+    ((0, 0), (1, 0), (3, 0), (2, 0), (3, 1), (2, 1), (0, 1), (1, 1)),
 )
 SENDS = (
     (
-        (10000, 10002, 10010, 10022, 10020, 10032, 10030, 11002, 10040, 11012, 10050, 11022, 10060, 10042,
-         10070, 10052, 11100, 12002, 10130, 12012, 12022, 10150),
-        (),
-        (12100, 11032),
-        (),
-        (11042, 20100, 20110, 12032, 20120, 12042),
-        (12052,),
-        (),
-        (),
-        (21100, 21132, 21110),
-        (),
-        (21120, 12062),
-        (),
-        (22112, 22000, 22122, 21000, 22132, 12072, 22010, 13002, 22020, 13012, 21010, 22030, 13022, 21020),
-        (),
-        (13042,),
-        (),
-        (21030, 22040, 22152),
-        (22172,),
-        (22100,),
-        (),
-        (20142,),
-        (20152,),
-        (22050, 20162),
-        (),
-        (22070, 23130, 23102),
-        (23030,),
-        (23122,),
-        (),
-        (23160, 23170, 11062, 11072, 23000, 23142, 23020, 23060, 23112, 23152),
-        (),
-        (23040, 20132),
-        (),
-        (23010, 20172, 23070, 23050, 22162, 21142, 22140, 21152, 30000, 21162, 30020, 22060, 21172, 30030,
-         21040, 30040, 21050, 30010, 21060, 30050, 21070, 30060, 30070),
+        (10003, 10002, 10032, 10023, 10045, 10100, 10043, 11005, 11025, 10143, 10063, 12005, 11100, 12025),
+        (),
+        (),
+        (),
+        (21122, 21103, 21130, 10065, 13002, 21003),
+        (),
+        (),
+        (),
+        (),
+        (22102, 22110, 22125, 22010),
+        (),
+        (13022,),
+        (),
+        (),
+        (22000,),
+        (),
+        (13045, 20170, 22023, 21023, 13065),
+        (),
+        (),
+        (),
+        (23102, 23110, 23122, 23130, 12045),
+        (),
+        (23003,),
+        (),
+        (23145, 23160, 23172, 23023, 20102),
+        (),
+        (),
+        (),
+        (23043, 22145, 22165, 23063, 20122),
+        (22043,),
+        (20112,),
+        (),
+        (21160, 21145, 22063, 21172, 21060, 20132, 20145, 30000, 30010, 21043, 20162, 30020, 21070, 30030,
+         30040, 30050, 30070, 30060),
     ),
     (
-        (11000, 11001, 11012, 11010, 11011, 11022, 11020, 11021, 11032, 11030, 12001, 10002, 11120, 12011,
-         10012, 11130, 12021, 10022, 12012, 10100, 12031, 11040, 10111, 10042, 11050, 11031, 11042, 11060,
-         11041, 10062, 11070, 12041, 10072, 10000, 12042, 12051),
-        (10010, 12052),
-        (10161,),
-        (11062,),
-        (10150, 10171, 10020, 12061, 11072, 10030, 12071, 13012, 11160, 13151, 13001, 13022, 11170, 10040,
-         13011, 13032, 13021, 21102, 10050, 21110),
-        (13131, 10060, 13031, 21122),
-        (13042,),
-        (10070, 13041),
-        (22152, 22172),
-        (12150,),
-        (13051,),
-        (),
-        (13062, 13061),
-        (),
-        (13072, 13071),
-        (),
-        (20110, 20102, 20122),
-        (13161,),
-        (20142, 11151),
-        (13171, 20152),
-        (11051, 22130, 22030),
-        (),
-        (11061,),
-        (22112,),
-        (11071, 22102),
-        (22122,),
-        (21141, 22050),
-        (),
-        (22070, 22000, 23102, 23111),
-        (23122, 21161),
-        (22010,),
-        (23132, 20131),
-        (22020, 23142, 20171, 23160, 31000, 23152, 22161, 31010, 23172, 23000, 31020, 23030, 23020, 20162,
-         21132, 20001, 21152, 23040, 20021, 21172, 23010, 20031, 23060, 23050, 20041, 31030, 23070, 20011,
-         22142, 20051, 22060, 20061, 22040, 20071, 31050, 31060, 31040, 31070),
+        (11003, 11004, 11012, 11025, 11023, 11024, 11045, 10003, 12004, 10012, 10023, 12024, 10025, 11120,
+         13005, 13004, 10111, 11065, 10043),
+        (10123, 10121, 12005),
+        (),
+        (13024,),
+        (13111, 10063, 13045, 11043),
+        (10065, 13044),
+        (13131,),
+        (11063,),
+        (),
+        (12032,),
+        (13064,),
+        (),
+        (23100, 12045, 12044, 10163, 23120, 12065, 12064),
+        (),
+        (20102,),
+        (11044,),
+        (22003, 22122),
+        (22103,),
+        (12164, 20122),
+        (22030, 21122),
+        (),
+        (23172, 11064),
+        (22020,),
+        (22130,),
+        (23112,),
+        (11144, 22160),
+        (23132,),
+        (23143, 22145),
+        (),
+        (20172, 11164),
+        (31020,),
+        (23003,),
+        (23162, 20111, 22172, 20131, 23023, 20161, 20145, 21105, 23043, 20004, 21132, 23063, 21145, 20024,
+         22043, 20044, 21165, 31000, 31010, 31030, 20064, 22063, 31040, 31050, 31060, 31070),
     ),
 )
 
@@ -108,34 +104,46 @@
 
 
 def digits(code):
-    return code // 10000, code // 1000 % 10, code // 100 % 10, code // 10 % 10, code % 10
+    way = code % 10
+    return code // 10000, code // 1000 % 10, code // 100 % 10, code // 10 % 10, 1 + way // 3, way % 3
 
 
 def script(depth):
-    acts, came = [], [{} for _ in SENDS]
+    tokens, results = [{} for _ in SENDS], [{} for _ in SENDS]
     for role, pieces in enumerate(SENDS):
-        seen, mine = set(), []
+        for kind, o, r, u, units, way in [digits(code) for piece in pieces for code in piece]:
+            there, o, r, way = role + (way == AWAY) - (way == HOME), o, r ^ (way == ACROSS), way
+            if there == depth // 2:
+                there, o, way = role, depth - 1 - o, HOME
+            for v in range(u, u + units):
+                if kind == 1:
+                    tokens[there][o, r, v] = (u, units)
+                if kind == 2:
+                    results[there].setdefault((o, r, v), []).append((way, u, units))
+    acts = []
+    for role, pieces in enumerate(SENDS):
+        seen, heard, mine = set(), set(), []
         for index, piece in enumerate(pieces):
             found = []
 
             def need(o, r, u):
                 if (o, r) != (role, 0) and (o, r, u) not in seen:
-                    seen.add((o, r, u))
-                    found.append((0, o, r, u, ACROSS))
-
-            for code in piece:
-                kind, o, r, u, way = digits(code)
-                if kind == 1:
-                    need(o, r, u)
-                found.append((kind, o, r, u, way))
-                if kind != 2:
-                    continue
-                there, key = role + (way == AWAY) - (way == HOME), (o, r, u)
-                if way == ACROSS:
-                    key = (o, 1 - r, u)
-                if there == depth // 2:
-                    there, key, way = role, (depth - 1 - o, r, u), HOME
-                came[there].setdefault(key, []).append(way)
+                    first, units = tokens[role][o, r, u]
+                    seen.update((o, r, first + v) for v in range(units))
+                    found.append((0, o, r, first, units, ACROSS, ()))
+
+            for kind, o, r, u, units, way in [digits(code) for code in piece]:
+                ways = []
+                for v in range(u, u + units):
+                    if kind == 1:
+                        need(o, r, v)
+                        continue
+                    for source, first, size in results[role].get((o, r, v), []):
+                        if (source, o, r, first) not in heard:
+                            heard.add((source, o, r, first))
+                            found.append((4, o, r, first, size, source, ()))
+                    ways.append(tuple(source for source, _, _ in results[role].get((o, r, v), [])))
+                found.append((kind, o, r, u, units, way, tuple(ways)))
             if index % PIECES == 0 and index < len(ROUNDS[role]) * PIECES:
                 o, h = ROUNDS[role][index // PIECES]
                 for r in range(SIDE):
@@ -143,7 +151,7 @@
                         need(o, r, u)
             mine.append(found)
         acts.append(mine)
-    return acts, came
+    return acts
 
 
 def kernel(
@@ -162,7 +170,7 @@
     size = count // UNITS
     half = count // 2
     spots = depth * SIDE * UNITS
-    acts, came = script(depth)
+    acts = script(depth)
     steps = len(ROUNDS[0])
 
     def owner_of(o):
@@ -192,19 +200,21 @@
             device_id={"ep": there}, device_id_type=pl.DeviceIdType.MESH,
         )
 
-    def token_copy(o, r, u, way):
-        ref = rows.at[cut(offset(o, r, u))]
+    def token_copy(o, r, u, units, way):
+        ref = rows.at[cut(offset(o, r, u), units * size)]
         return remote(ref, ref, token_send.at[way], token_recv.at[spot(o, r, u)], device(way))
 
-    def landing(o, r, u, way):
+    def landing(o, r, u, units, way):
         if way == ACROSS:
-            return side.at[cut(owner_of(o) * count + u * size)], side_recv.at[owner_of(o) * UNITS + u]
+            start, recv = owner_of(o) * count + u * size, side_recv.at[owner_of(o) * UNITS + u]
+            return side.at[cut(start, units * size)], recv
         start = heading(way) * (depth * SIDE * count) + offset(o, r, u)
-        return line.at[cut(start)], line_recv.at[heading(way) * spots + spot(o, r, u)]
-
-    def result_copy(o, r, u, way):
-        target, recv = landing(o, r, u, way)
-        return remote(part.at[cut(offset(o, r, u))], target, result_send.at[way], recv, device(way))
+        return line.at[cut(start, units * size)], line_recv.at[heading(way) * spots + spot(o, r, u)]
+
+    def result_copy(o, r, u, units, way):
+        target, recv = landing(o, r, u, units, way)
+        source = part.at[cut(offset(o, r, u), units * size)]
+        return remote(source, target, result_send.at[way], recv, device(way))
 
     own = []
     for h in range(2):
@@ -228,51 +238,48 @@
         )
 
     gates = nums[...].astype(jnp.float32) / denominator
-    lanes = lax.broadcasted_iota(jnp.int32, weights.shape[1:], 0)
     for d in range(n):
-        block = jnp.zeros(weights.shape[1:], jnp.float32)
         for e in range(local):
-            chosen = jnp.sum(jnp.where(ids[...] == d * local + e, gates, 0.0), axis=0, keepdims=True)
-            block = jnp.where(lanes == e, chosen, block)
-        weights[d] = block
+            chosen = jnp.where(ids[...] == d * local + e, gates, 0.0)
+            weights[d, e : e + 1] = jnp.sum(chosen, axis=0, keepdims=True)
     factors[me] = weights[me]
 
     pl.semaphore_wait(barrier, n - 1)
     for load in own:
         load.wait()
 
-    def act(role, kind, o, r, u, way):
+    def added(o, r, u, units, ways):
+        total = part[cut(offset(o, r, u), units * size)].astype(jnp.float32)
+        for way in ways:
+            total = total + landing(o, r, u, units, way)[0][...].astype(jnp.float32)
+        return total
+
+    def act(kind, o, r, u, units, way, ways):
         if kind == 0:
-            token_copy(o, r, u, way).wait_recv()
-            return
-        if kind == 1:
-            token_copy(o, r, u, way).start()
-            return
-        if kind == 3:
-            o, r = role, 0
-        mine = part.at[cut(offset(o, r, u))]
-        ways = came[role].get((o, r, u), [])
-        if ways:
-            total = mine[...].astype(jnp.float32)
-            for source in ways:
-                target, recv = landing(o, r, u, source)
-                remote(target, target, result_send.at[source], recv, device(source)).wait_recv()
-                total = total + target[...].astype(jnp.float32)
-            if kind == 2:
-                mine[...] = total.astype(part.dtype)
-        if kind == 2:
-            result_copy(o, r, u, way).start()
+            token_copy(o, r, u, units, way).wait_recv()
+        elif kind == 1:
+            token_copy(o, r, u, units, way).start()
+        elif kind == 4:
+            target, recv = landing(o, r, u, units, way)
+            remote(target, target, result_send.at[way], recv, device(way)).wait_recv()
+        elif kind == 3:
+            out[pl.ds(u * size, size)] = added(o, r, u, units, ways[0]).astype(out.dtype)
         else:
-            out[pl.ds(u * size, size)] = total.astype(out.dtype)
+            together = units if len(set(ways)) == 1 else 1
+            for v in range(0, units, together):
+                if ways[v]:
+                    total = added(o, r, u + v, together, ways[v])
+                    part[cut(offset(o, r, u + v), together * size)] = total.astype(part.dtype)
+            result_copy(o, r, u, units, way).start()
 
     def talk(p, i):
         for role, pieces in enumerate(acts):
             for step in range(steps):
                 piece = pieces[step * PIECES + p]
 
-                def body(role=role, piece=piece):
+                def body(piece=piece):
                     for action in piece:
-                        act(role, *action)
+                        act(*action)
 
                 if piece:
                     pl.when((place == role) & (i == step))(body)
@@ -298,7 +305,7 @@
             there = factors.at[source]
             remote(there, there, weight_send.at[0], weight_recv.at[source], source).wait_recv()
         for d in range(n):
-            turned = factors[d].T
+            turned = jnp.concatenate([factors[d], jnp.zeros((-local % 8, count), jnp.float32)], axis=0).T
             for h in range(2):
                 start = d // SIDE * SIDE * count + h * count + d % SIDE * half
                 columns[pl.ds(start, half)] = turned[h * half : (h + 1) * half]
@@ -352,10 +359,10 @@
     def ending(role):
         for piece in acts[role][steps * PIECES :]:
             for action in piece:
-                act(role, *action)
+                act(*action)
         for way in (AWAY, HOME, ACROSS):
             for kind, sems in ((1, token_send), (2, result_send)):
-                sent = sum(a[0] == kind and a[4] == way for piece in acts[role] for a in piece)
+                sent = sum(a[4] for piece in acts[role] for a in piece if a[0] == kind and a[5] == way)
                 if sent:
                     all_of = rows.at[pl.ds(0, sent * size)]
                     remote(all_of, all_of, sems.at[way], token_recv.at[0], device(way)).wait_send()
@@ -382,9 +389,9 @@
         out_specs=vmem,
         scratch_shapes=[
             pltpu.VMEM((everyone, width), kind),
-            pltpu.VMEM((n, 8, count), jnp.float32),
-            pltpu.VMEM((n, 8, count), jnp.float32),
-            pltpu.VMEM((everyone, 8), jnp.float32),
+            pltpu.VMEM((n, local, count), jnp.float32),
+            pltpu.VMEM((n, local, count), jnp.float32),
+            pltpu.VMEM((everyone, local + -local % 8), jnp.float32),
             pltpu.VMEM((local, width, ff), kind),
             pltpu.VMEM((local, width, ff), kind),
             pltpu.VMEM((local * ff, width), kind),

time: 88.5 us -> 77.2 us (0.87)
  Pallas kernels: 86.4 us -> 75.1 us
    pallas_call x1, Pallas kernels: 86.4 us -> 75.1 us  [fused(): pl.pallas_call(functools.partial(kernel, n, local), out_shape=jax.ShapeDt...]
where the time goes in v2:
time: 77.2 us; the launch traced here: 77 us
  Pallas kernels  75.1 us (97%)
  local copies, waits for them, and re-layouts  1.88 us (2%)
    pallas_call x1, Pallas kernels, fused(): pl.pallas_call(functools.partial(kernel, n, local), out_shape=jax.ShapeDt...  75.1 us
    unnamed x1, local copies, waits for them, and re-layouts  1.88 us

profile of v2, /device:TPU:0, one launch (start us, length us, event | category | flops | bytes accessed | tf_op | source)
XLA Modules:
  0.0 77.0 jit_solution(6109556214561687109)
XLA Ops:
  0.0 75.1 %shard_map.64 = bf16[128,2048]{1,0:T(8,128)(2,1)} custom-call(s32[8,128]{1,0:T(8,128)} %bitcast.2, s32[8,128]{1,0:T(8,128)} %bitcast.3, bf16[128,2048]{1,0:T(8,128)(2,1)} %tokens.1, bf16[2,2048,768]{2,1,0:T(8,128)(2,1)} %w_gate.1, bf16[2,2048,768]{2,1,0:T(8,128)(2,1)} %w_up.1, bf16[2,768,2048]{2,1,0:T(8,128)(2,1)} %w_down.1), custom_call_target="tpu_custom_call" | custom-call | tf_op jit(solution)/shard_map/pallas_call | solution.py:385
  75.1 1.9 %copy.8 = bf16[128,2048]{1,0:T(8,128)(2,1)} copy(bf16[128,2048]{1,0:T(8,128)(2,1)} %shard_map.64) | data formatting | bytes 1048576

commit v3 on v2

--- a/solution.py
+++ b/solution.py
@@ -10,7 +10,7 @@
 denominator = 1024.0
 SIDE = 2
 LANES = 256
-VMEM = 60 * 2**20
+VMEM = 53 * 2**20
 
 AWAY, HOME, ACROSS = 0, 1, 2
 UNITS = 8
@@ -21,7 +21,8 @@
 )
 SENDS = (
     (
-        (10003, 10002, 10032, 10023, 10045, 10100, 10043, 11005, 11025, 10143, 10063, 12005, 11100, 12025),
+        (50000, 10003, 10002, 10032, 10023, 10045, 10100, 10043, 51000, 11005, 11025, 10143, 52000, 10063,
+         12005, 11100, 53000, 12025),
         (),
         (),
         (),
@@ -57,8 +58,8 @@
          30040, 30050, 30070, 30060),
     ),
     (
-        (11003, 11004, 11012, 11025, 11023, 11024, 11045, 10003, 12004, 10012, 10023, 12024, 10025, 11120,
-         13005, 13004, 10111, 11065, 10043),
+        (51000, 11003, 11004, 11012, 11025, 11023, 11024, 11045, 50000, 52000, 10003, 12004, 10012, 10023,
+         12024, 10025, 11120, 53000, 13005, 13004, 10111, 11065, 10043),
         (10123, 10121, 12005),
         (),
         (13024,),
@@ -137,6 +138,7 @@
                 for v in range(u, u + units):
                     if kind == 1:
                         need(o, r, v)
+                    if kind not in (2, 3):
                         continue
                     for source, first, size in results[role].get((o, r, v), []):
                         if (source, o, r, first) not in heard:
@@ -146,6 +148,8 @@
                 found.append((kind, o, r, u, units, way, tuple(ways)))
             if index % PIECES == 0 and index < len(ROUNDS[role]) * PIECES:
                 o, h = ROUNDS[role][index // PIECES]
+                if o not in [entry[0] for entry in ROUNDS[role][: index // PIECES]]:
+                    found.append((6, o, 0, 0, 0, 0, ()))
                 for r in range(SIDE):
                     for u in range(h * UNITS // 2, (h + 1) * UNITS // 2):
                         need(o, r, u)
@@ -157,8 +161,8 @@
 def kernel(
     n, local,
     ids, nums, tokens, w_gate, w_up, w_down, out,
-    rows, weights, factors, columns, gate, up, down, hidden, part, line, side,
-    load_sem, weight_send, weight_recv, token_send, token_recv, result_send, line_recv, side_recv,
+    rows, shares, factors, columns, gate, up, down, hidden, part, line, side,
+    load_sem, share_send, share_recv, factor_send, factor_recv, token_send, token_recv, result_send, line_recv, side_recv,
 ):
     depth = n // SIDE
     me = lax.axis_index("ep")
@@ -232,19 +236,21 @@
         load.start()
 
     barrier = pltpu.get_barrier_semaphore()
-    for k in range(1, n):
-        pl.semaphore_signal(
-            barrier, inc=1, device_id={"ep": (me + k) % n}, device_id_type=pl.DeviceIdType.MESH
-        )
+    def greet(there):
+        pl.semaphore_signal(barrier, inc=1, device_id={"ep": there}, device_id_type=pl.DeviceIdType.MESH)
+
+    greet(device(ACROSS))
+    greet(device(AWAY))
+    pl.when(place > 0)(lambda: greet(device(HOME)))
 
     gates = nums[...].astype(jnp.float32) / denominator
     for d in range(n):
         for e in range(local):
             chosen = jnp.where(ids[...] == d * local + e, gates, 0.0)
-            weights[d, e : e + 1] = jnp.sum(chosen, axis=0, keepdims=True)
-    factors[me] = weights[me]
-
-    pl.semaphore_wait(barrier, n - 1)
+            shares[z * n + d, e : e + 1] = jnp.sum(chosen, axis=0, keepdims=True)
+
+    pl.when(place == 0)(lambda: pl.semaphore_wait(barrier, 2))
+    pl.when(place > 0)(lambda: pl.semaphore_wait(barrier, 3))
     for load in own:
         load.wait()
 
@@ -254,7 +260,43 @@
             total = total + landing(o, r, u, units, way)[0][...].astype(jnp.float32)
         return total
 
-    def act(kind, o, r, u, units, way, ways):
+    def onward(role, o):
+        return [AWAY] * (o <= role) + [HOME] * (o >= role and role > 0)
+
+    def beyond(role, way):
+        return SIDE * (depth - 1 - role if way == AWAY else role)
+
+    def share_copy(role, o, way):
+        first = SIDE * (z + 1) if way == AWAY else 0
+        mirrored = 0 if way == AWAY else SIDE * (z + 1)
+        ref = shares.at[pl.ds(owner_of(o) * n + jnp.where(flip == 0, first, mirrored), beyond(role, way))]
+        return remote(ref, ref, share_send.at[0], share_recv.at[owner_of(o)], device(way))
+
+    def factor_copy(o):
+        there = device(ACROSS)
+        return remote(
+            shares.at[owner_of(o) * n + there], factors.at[owner_of(o)], factor_send.at[0], factor_recv.at[owner_of(o)], there
+        )
+
+    def pass_on(role, o):
+        if o != role:
+            extent = SIDE * (depth - role if o < role else role + 1)
+            start = jnp.where((flip == 0) == (o < role), SIDE * z, 0)
+            ref = shares.at[pl.ds(owner_of(o) * n + start, extent)]
+            remote(ref, ref, share_send.at[0], share_recv.at[owner_of(o)], device(ACROSS)).wait_recv()
+        for way in onward(role, o):
+            share_copy(role, o, way).start()
+        factor_copy(o).start()
+
+    def lay_out(o):
+        factor_copy(o).wait_recv()
+        for r, block in ((0, shares[owner_of(o) * n + me]), (1, factors[owner_of(o)])):
+            turned = jnp.concatenate([block, jnp.zeros((-local % 8, count), jnp.float32)], axis=0).T
+            for h in range(2):
+                start = owner_of(o) * SIDE * count + h * count + row_of(r) * half
+                columns[cut(start, half)] = turned[h * half : (h + 1) * half]
+
+    def act(role, kind, o, r, u, units, way, ways):
         if kind == 0:
             token_copy(o, r, u, units, way).wait_recv()
         elif kind == 1:
@@ -262,6 +304,10 @@
         elif kind == 4:
             target, recv = landing(o, r, u, units, way)
             remote(target, target, result_send.at[way], recv, device(way)).wait_recv()
+        elif kind == 5:
+            pass_on(role, o)
+        elif kind == 6:
+            lay_out(o)
         elif kind == 3:
             out[pl.ds(u * size, size)] = added(o, r, u, units, ways[0]).astype(out.dtype)
         else:
@@ -277,9 +323,9 @@
             for step in range(steps):
                 piece = pieces[step * PIECES + p]
 
-                def body(piece=piece):
+                def body(role=role, piece=piece):
                     for action in piece:
-                        act(*action)
+                        act(role, *action)
 
                 if piece:
                     pl.when((place == role) & (i == step))(body)
@@ -291,24 +337,6 @@
                 if entry[which]:
                     found = found + jnp.where((place == role) & (i == step), entry[which], 0)
         return found
-
-    def weight_copy(k):
-        there = (me + k) % n
-        return remote(weights.at[there], factors.at[me], weight_send.at[0], weight_recv.at[me], there)
-
-    for k in range(1, n):
-        weight_copy(k).start()
-
-    def ready():
-        for k in range(1, n):
-            source = (me + k) % n
-            there = factors.at[source]
-            remote(there, there, weight_send.at[0], weight_recv.at[source], source).wait_recv()
-        for d in range(n):
-            turned = jnp.concatenate([factors[d], jnp.zeros((-local % 8, count), jnp.float32)], axis=0).T
-            for h in range(2):
-                start = d // SIDE * SIDE * count + h * count + d % SIDE * half
-                columns[pl.ds(start, half)] = turned[h * half : (h + 1) * half]
 
     def project(e, base):
         column = columns[cut(base, count), e : e + 1]
@@ -342,8 +370,6 @@
 
             @pl.when(i == 0)
             def _():
-                if p == 0:
-                    ready()
                 for load in loads[2 * p : 2 * p + 2] if p < local else loads[2 * local :] if p == local else []:
                     load.wait()
 
@@ -359,7 +385,7 @@
     def ending(role):
         for piece in acts[role][steps * PIECES :]:
             for action in piece:
-                act(*action)
+                act(role, *action)
         for way in (AWAY, HOME, ACROSS):
             for kind, sems in ((1, token_send), (2, result_send)):
                 sent = sum(a[4] for piece in acts[role] for a in piece if a[0] == kind and a[5] == way)
@@ -367,10 +393,13 @@
                     all_of = rows.at[pl.ds(0, sent * size)]
                     remote(all_of, all_of, sems.at[way], token_recv.at[0], device(way)).wait_send()
 
+        passed = sum(beyond(role, way) for o in range(depth) for way in onward(role, o))
+        given = shares.at[pl.ds(0, passed)]
+        remote(given, given, share_send.at[0], share_recv.at[0], device(ACROSS)).wait_send()
+
     for role in range(len(acts)):
         pl.when(place == role)(functools.partial(ending, role))
-    given = weights.at[pl.ds(0, n - 1)]
-    remote(given, given, weight_send.at[0], weight_recv.at[0], device(ACROSS)).wait_send()
+    remote(factors, factors, factor_send.at[0], factor_recv.at[0], device(ACROSS)).wait_send()
 
 
 def fused(tokens, expert_ids, gate_nums, w_gate, w_up, w_down, n):
@@ -389,8 +418,8 @@
         out_specs=vmem,
         scratch_shapes=[
             pltpu.VMEM((everyone, width), kind),
-            pltpu.VMEM((n, local, count), jnp.float32),
-            pltpu.VMEM((n, local, count), jnp.float32),
+            pltpu.VMEM((depth * n, local, count), jnp.float32),
+            pltpu.VMEM((depth, local, count), jnp.float32),
             pltpu.VMEM((everyone, local + -local % 8), jnp.float32),
             pltpu.VMEM((local, width, ff), kind),
             pltpu.VMEM((local, width, ff), kind),
@@ -400,7 +429,7 @@
             pltpu.VMEM((2 * everyone, width), kind),
             pltpu.VMEM((depth * count, width), kind),
             dma((2 + 3 * local,)),
-            dma((1,)), dma((n,)),
+            dma((1,)), dma((depth,)), dma((1,)), dma((depth,)),
             dma((3,)), dma((n * UNITS,)),
             dma((3,)), dma((2 * n * UNITS,)), dma((depth * UNITS,)),
         ],

time: 77.2 us -> 74.4 us (0.964)
  Pallas kernels: 75.1 us -> 72 us
    pallas_call x1, Pallas kernels: 75.1 us -> 72 us  [fused(): pl.pallas_call(functools.partial(kernel, n, local), out_shape=jax.ShapeDt...]
    unnamed x1 -> x5, local copies, waits for them, and re-layouts: 1.88 us -> 2.17 us
where the time goes in v3:
time: 74.4 us; the launch traced here: 74.1 us
  Pallas kernels  72 us (97%)
  local copies, waits for them, and re-layouts  2.17 us (3%)
    pallas_call x1, Pallas kernels, fused(): pl.pallas_call(functools.partial(kernel, n, local), out_shape=jax.ShapeDt...  72 us
    unnamed x5, local copies, waits for them, and re-layouts  2.17 us

profile of v3, /device:TPU:0, one launch (start us, length us, event | category | flops | bytes accessed | tf_op | source)
XLA Modules:
  0.0 74.1 jit_solution(15194977174211142551)
XLA Ops:
  0.0 0.0 copy-start
  0.0 0.7 copy-done
  0.7 0.0 copy-start.1
  0.7 0.7 copy-done.1
  1.4 72.0 %shard_map.64 = bf16[128,2048]{1,0:T(8,128)(2,1)S(1)} custom-call(s32[8,128]{1,0:T(8,128)S(1)} %bitcast.2, s32[8,128]{1,0:T(8,128)S(1)} %bitcast.3, bf16[128,2048]{1,0:T(8,128)(2,1)} %tokens.1, bf16[2,2048,768]{2,1,0:T(8,128)(2,1)} %w_gate.1, bf16[2,2048,768]{2,1,0:T(8,128)(2,1)} %w_up.1, bf16[2,768,2048]{2,1,0:T(8,128)(2,1)} %w_down.1), custom_call_target="tpu_custom_call" | custom-call | tf_op jit(solution)/shard_map/pallas_call | solution.py:414
  73.3 0.8 %copy.8 = bf16[128,2048]{1,0:T(8,128)(2,1)} copy(bf16[128,2048]{1,0:T(8,128)(2,1)S(1)} %shard_map.64) | data formatting | bytes 1048576
Async XLA Ops:
  0.0 0.7 copy-start
  0.7 0.7 copy-start.1

commit v4 on v3

--- a/solution.py
+++ b/solution.py
@@ -21,78 +21,79 @@
 )
 SENDS = (
     (
-        (50000, 10003, 10002, 10032, 10023, 10045, 10100, 10043, 51000, 11005, 11025, 10143, 52000, 10063,
-         12005, 11100, 53000, 12025),
-        (),
-        (),
-        (),
-        (21122, 21103, 21130, 10065, 13002, 21003),
-        (),
-        (),
-        (),
-        (),
-        (22102, 22110, 22125, 22010),
-        (),
-        (13022,),
-        (),
-        (),
-        (22000,),
-        (),
-        (13045, 20170, 22023, 21023, 13065),
-        (),
-        (),
-        (),
-        (23102, 23110, 23122, 23130, 12045),
-        (),
-        (23003,),
-        (),
-        (23145, 23160, 23172, 23023, 20102),
-        (),
-        (),
-        (),
-        (23043, 22145, 22165, 23063, 20122),
-        (22043,),
-        (20112,),
-        (),
-        (21160, 21145, 22063, 21172, 21060, 20132, 20145, 30000, 30010, 21043, 20162, 30020, 21070, 30030,
-         30040, 30050, 30070, 30060),
+        (500010, 100020, 100012, 100312, 100220, 100422, 101010, 100420, 510010, 110022, 110222, 101420,
+         520010, 100620, 120022, 111010, 530010, 120222),
+        (),
+        (),
+        (),
+        (211212, 211020, 211310, 100622, 130012, 210020),
+        (),
+        (),
+        (),
+        (),
+        (221012, 221110, 221222, 220110),
+        (),
+        (130212,),
+        (),
+        (),
+        (220010,),
+        (),
+        (130422, 201710, 220220, 210220, 130622),
+        (),
+        (),
+        (),
+        (231012, 231110, 231212, 231310, 120422),
+        (),
+        (230020,),
+        (),
+        (231422, 231610, 231712, 230220, 201012),
+        (),
+        (),
+        (),
+        (230420, 221422, 221622, 230620, 201212),
+        (220420,),
+        (201112,),
+        (),
+        (211610, 211422, 220620, 211712, 210610, 201312, 201422, 300010, 300110, 210420, 201612, 300210,
+         210710, 300310, 300410, 300510, 300710, 300610),
     ),
     (
-        (51000, 11003, 11004, 11012, 11025, 11023, 11024, 11045, 50000, 52000, 10003, 12004, 10012, 10023,
-         12024, 10025, 11120, 53000, 13005, 13004, 10111, 11065, 10043),
-        (10123, 10121, 12005),
-        (),
-        (13024,),
-        (13111, 10063, 13045, 11043),
-        (10065, 13044),
-        (13131,),
-        (11063,),
-        (),
-        (12032,),
-        (13064,),
-        (),
-        (23100, 12045, 12044, 10163, 23120, 12065, 12064),
-        (),
-        (20102,),
-        (11044,),
-        (22003, 22122),
-        (22103,),
-        (12164, 20122),
-        (22030, 21122),
-        (),
-        (23172, 11064),
-        (22020,),
-        (22130,),
-        (23112,),
-        (11144, 22160),
-        (23132,),
-        (23143, 22145),
-        (),
-        (20172, 11164),
-        (31020,),
-        (23003,),
-        (23162, 20111, 22172, 20131, 23023, 20161, 20145, 21105, 23043, 20004, 21132, 23063, 21145, 20024,
-         22043, 20044, 21165, 31000, 31010, 31030, 20064, 22063, 31040, 31050, 31060, 31070),
+        (510010, 110020, 110021, 110112, 110222, 110220, 110221, 110422, 500010, 520010, 100020, 120021,
+         100112, 100220, 120221, 100222, 111210, 530010, 130022, 130021, 101111, 110622, 100420),
+        (101220, 101211, 120022),
+        (),
+        (130221,),
+        (131111, 100620, 130422, 110420),
+        (100622, 130421),
+        (131311,),
+        (110620,),
+        (),
+        (120312,),
+        (130621,),
+        (),
+        (231010, 120422, 120421, 101620, 231210, 120622, 120621),
+        (),
+        (201012,),
+        (110421,),
+        (220020, 221212),
+        (221020,),
+        (121621, 201212),
+        (220310, 211212),
+        (),
+        (231712, 110621),
+        (220210,),
+        (221310,),
+        (231112,),
+        (111421, 221610),
+        (231312,),
+        (231420, 221422),
+        (),
+        (201712, 111621),
+        (310210,),
+        (230020,),
+        (231612, 201111, 221712, 201311, 230220, 201611, 201422, 211022, 230420, 200021, 211312, 230620,
+         211422, 200221, 220420, 200421, 211622, 310010, 310110, 310310, 200621, 220620, 310410, 310510,
+         310610, 310710),
     ),
 )
 
@@ -105,8 +106,7 @@
 
 
 def digits(code):
-    way = code % 10
-    return code // 10000, code // 1000 % 10, code // 100 % 10, code // 10 % 10, 1 + way // 3, way % 3
+    return tuple(code // 10**k % 10 for k in range(5, -1, -1))
 
 
 def script(depth):
@@ -160,7 +160,7 @@
 
 def kernel(
     n, local,
-    ids, nums, tokens, w_gate, w_up, w_down, out,
+    choices, tokens, w_gate, w_up, w_down, out,
     rows, shares, factors, columns, gate, up, down, hidden, part, line, side,
     load_sem, share_send, share_recv, factor_send, factor_recv, token_send, token_recv, result_send, line_recv, side_recv,
 ):
@@ -220,6 +220,14 @@
         source = part.at[cut(offset(o, r, u), units * size)]
         return remote(source, target, result_send.at[way], recv, device(way))
 
+    barrier = pltpu.get_barrier_semaphore()
+    def greet(there):
+        pl.semaphore_signal(barrier, inc=1, device_id={"ep": there}, device_id_type=pl.DeviceIdType.MESH)
+
+    greet(device(ACROSS))
+    greet(device(AWAY))
+    pl.when(place > 0)(lambda: greet(device(HOME)))
+
     own = []
     for h in range(2):
         start = z * SIDE * count + h * count + y * half
@@ -235,18 +243,11 @@
     for load in own + loads:
         load.start()
 
-    barrier = pltpu.get_barrier_semaphore()
-    def greet(there):
-        pl.semaphore_signal(barrier, inc=1, device_id={"ep": there}, device_id_type=pl.DeviceIdType.MESH)
-
-    greet(device(ACROSS))
-    greet(device(AWAY))
-    pl.when(place > 0)(lambda: greet(device(HOME)))
-
-    gates = nums[...].astype(jnp.float32) / denominator
+    ids = choices[...] // int(denominator)
+    gates = (choices[...] % int(denominator)).astype(jnp.float32) / denominator
     for d in range(n):
         for e in range(local):
-            chosen = jnp.where(ids[...] == d * local + e, gates, 0.0)
+            chosen = jnp.where(ids == d * local + e, gates, 0.0)
             shares[z * n + d, e : e + 1] = jnp.sum(chosen, axis=0, keepdims=True)
 
     pl.when(place == 0)(lambda: pl.semaphore_wait(barrier, 2))
@@ -407,6 +408,7 @@
     local, _, ff = w_gate.shape
     depth = n // SIDE
     everyone = n * count
+    choices = (expert_ids * int(denominator) + gate_nums).T
     kind = tokens.dtype
     dma = pltpu.SemaphoreType.DMA
     vmem = pl.BlockSpec(memory_space=pltpu.VMEM)
@@ -414,7 +416,7 @@
     return pl.pallas_call(
         functools.partial(kernel, n, local),
         out_shape=jax.ShapeDtypeStruct((count, width), kind),
-        in_specs=[vmem, vmem, hbm, hbm, hbm, hbm],
+        in_specs=[vmem, hbm, hbm, hbm, hbm],
         out_specs=vmem,
         scratch_shapes=[
             pltpu.VMEM((everyone, width), kind),
@@ -436,7 +438,7 @@
         compiler_params=pltpu.CompilerParams(
             collective_id=0, has_side_effects=True, vmem_limit_bytes=VMEM
         ),
-    )(expert_ids.T, gate_nums.T, tokens, w_gate, w_up, w_down)
+    )(choices, tokens, w_gate, w_up, w_down)
 
 
 def plain(tokens, expert_ids, gate_nums, w_gate, w_up, w_down, n):

time: 74.4 us -> 73.7 us (level)
  local copies, waits for them, and re-layouts: 2.17 us -> 0.8 us
    unnamed x5 -> x1, local copies, waits for them, and re-layouts: 2.17 us -> 0.8 us
where the time goes in v4:
time: 73.7 us; the launch traced here: 73.4 us
  Pallas kernels  71.9 us (98%)
  local copies, waits for them, and re-layouts  0.8 us (1%)
    pallas_call x1, Pallas kernels, fused(): pl.pallas_call(functools.partial(kernel, n, local), out_shape=jax.ShapeDt...  71.9 us

profile of v4, /device:TPU:0, one launch (start us, length us, event | category | flops | bytes accessed | tf_op | source)
XLA Modules:
  0.0 73.4 jit_solution(14929170828926607265)
XLA Ops:
  0.0 0.7 add_bitcast_fusion.choices
  0.7 71.9 %shard_map.64 = bf16[128,2048]{1,0:T(8,128)(2,1)S(1)} custom-call(s32[8,128]{1,0:T(8,128)S(1)} %add_bitcast_fusion.choices, bf16[128,2048]{1,0:T(8,128)(2,1)} %tokens.1, bf16[2,2048,768]{2,1,0:T(8,128)(2,1)} %w_gate.1, bf16[2,2048,768]{2,1,0:T(8,128)(2,1)} %w_up.1, bf16[2,768,2048]{2,1,0:T(8,128)(2,1)} %w_down.1), custom_call_target="tpu_custom_call" | custom-call | tf_op jit(solution)/shard_map/pallas_call | solution.py:416
  72.6 0.8 %copy.8 = bf16[128,2048]{1,0:T(8,128)(2,1)} copy(bf16[128,2048]{1,0:T(8,128)(2,1)S(1)} %shard_map.64) | data formatting | bytes 1048576

commit v5 on v4

--- a/solution.py
+++ b/solution.py
@@ -319,25 +319,39 @@
                     part[cut(offset(o, r, u + v), together * size)] = total.astype(part.dtype)
             result_copy(o, r, u, units, way).start()
 
+    def branch(index, low, high, todo):
+        if not any(k in todo for k in range(low, high)):
+            return
+        if high - low == 1:
+            todo[low]()
+            return
+        mid = (low + high) // 2
+        lax.cond(
+            index < mid, lambda: branch(index, low, mid, todo), lambda: branch(index, mid, high, todo)
+        )
+
     def talk(p, i):
-        for role, pieces in enumerate(acts):
-            for step in range(steps):
-                piece = pieces[step * PIECES + p]
-
-                def body(role=role, piece=piece):
-                    for action in piece:
-                        act(role, *action)
-
-                if piece:
-                    pl.when((place == role) & (i == step))(body)
-
-    def pick(i, which):
-        found = jnp.int32(0)
-        for role, rounds in enumerate(ROUNDS):
-            for step, entry in enumerate(rounds):
-                if entry[which]:
-                    found = found + jnp.where((place == role) & (i == step), entry[which], 0)
-        return found
+        def speak(role, piece):
+            for action in piece:
+                act(role, *action)
+
+        def in_role(role):
+            found = {k: acts[role][k * PIECES + p] for k in range(steps)}
+            branch(i, 0, steps, {k: functools.partial(speak, role, piece) for k, piece in found.items() if piece})
+
+        branch(place, 0, len(acts), {role: functools.partial(in_role, role) for role in range(len(acts))})
+
+    def pick(i):
+        def halve(index, low, high, value):
+            if high - low == 1:
+                return value(low)
+            mid = (low + high) // 2
+            return jnp.where(index < mid, halve(index, low, mid, value), halve(index, mid, high, value))
+
+        def in_role(role):
+            return halve(i, 0, steps, lambda k: jnp.int32(ROUNDS[role][k][0] * 2 + ROUNDS[role][k][1]))
+
+        return halve(place, 0, len(ROUNDS), in_role)
 
     def project(e, base):
         column = columns[cut(base, count), e : e + 1]
@@ -363,7 +377,8 @@
         lax.fori_loop(low, high, tile, 0, unroll=True)
 
     def step(i, carry):
-        o, h = pick(i, 0), pick(i, 1)
+        code = pick(i)
+        o, h = code // 2, code % 2
         base = owner_of(o) * SIDE * count + h * count
         tiles = width // LANES
         for p in range(PIECES):

time: 73.7 us -> 72.8 us (0.988)
  Pallas kernels: 71.9 us -> 71 us
    pallas_call x1, Pallas kernels: 71.9 us -> 71 us  [fused(): pl.pallas_call(functools.partial(kernel, n, local), out_shape=jax.ShapeDt...]
where the time goes in v5:
time: 72.8 us; the launch traced here: 72.5 us
  Pallas kernels  71 us (98%)
  local copies, waits for them, and re-layouts  0.8 us (1%)
    pallas_call x1, Pallas kernels, fused(): pl.pallas_call(functools.partial(kernel, n, local), out_shape=jax.ShapeDt...  71 us

profile of v5, /device:TPU:0, one launch (start us, length us, event | category | flops | bytes accessed | tf_op | source)
XLA Modules:
  0.0 72.5 jit_solution(6322561372055053967)
XLA Ops:
  0.0 0.7 add_bitcast_fusion.choices
  0.7 71.0 %shard_map.64 = bf16[128,2048]{1,0:T(8,128)(2,1)S(1)} custom-call(s32[8,128]{1,0:T(8,128)S(1)} %add_bitcast_fusion.choices, bf16[128,2048]{1,0:T(8,128)(2,1)} %tokens.1, bf16[2,2048,768]{2,1,0:T(8,128)(2,1)} %w_gate.1, bf16[2,2048,768]{2,1,0:T(8,128)(2,1)} %w_up.1, bf16[2,768,2048]{2,1,0:T(8,128)(2,1)} %w_down.1), custom_call_target="tpu_custom_call" | custom-call | tf_op jit(solution)/shard_map/pallas_call | solution.py:431
  71.8 0.8 %copy.8 = bf16[128,2048]{1,0:T(8,128)(2,1)} copy(bf16[128,2048]{1,0:T(8,128)(2,1)S(1)} %shard_map.64) | data formatting | bytes 1048576
